TPU v7x, 768 devices: a whole 4x8x12 slice. The times are simulated.
768 devices in a mesh: dp: 12 (over z), rep: 8 (over y), grp: 8 (over x, core).
Axes of the slice: x: 4, y: 8, z: 12, core: 2. Of those that a mesh axis runs over, the one named last changes fastest.
Arguments:
- grad_parts: float32 [64, 24, 192, 2048], P(('rep', 'grp'), None, 'dp'), may hold values from -16 to 16
- momentum: float32 [24, 192, 2048], P(None, 'dp', ('rep', 'grp')), may hold values from -24 to 24
- layer_live: int32 [24], replicated, may hold values from 0 to 1, as said below
Outputs:
- new_momentum: float32 [24, 192, 2048], P(None, 'dp', ('rep', 'grp'))
- orth_update: bfloat16 [24, 192, 2048], P(None, 'dp', ('rep', 'grp'))
Inputs may be any that keep to these rules, and one draw needn't show every extreme that they name: `layer_live`: at least one matrix is live in every draw.
All inputs are finite; a program needn't handle non-finite values.
Results may differ from a plain program's by a relative error of at most 0.028.
Values may be sent and summed in bfloat16 or wider, within the bound.
No kernel may reach another device: no remote copies, remote signals or barrier semaphores. Data moves between devices by JAX's collectives and lax.ppermute only.
A program may use at most 64 MiB of HBM per device.

v0:
```python
import functools
import math

import jax
import jax.numpy as jnp
from jax import lax
from jax.experimental import pallas as pl
from jax.experimental.pallas import tpu as pltpu
from jax.sharding import Mesh
from jax.sharding import PartitionSpec as P

ITERS = 5
COLS = ("rep", "x1", "x0", "c")
CHIPS = ("rep", "x1", "x0")
OWNERS = ("rep", "x1")

decay_rate = 0.95
first_coef = 3.4445
second_coef = -4.775
third_coef = 2.0315
norm_eps = 1e-07

bf16 = jnp.bfloat16
f32 = jnp.float32
i32 = jnp.int32


def whole(space=pltpu.VMEM):
    return pl.BlockSpec(memory_space=space)


def room(mib):
    return pltpu.CompilerParams(vmem_limit_bytes=mib << 20)


def halves(a):
    high = a.astype(bf16)
    return high, (a - high.astype(f32)).astype(bf16)


def dot(a, b):
    return jnp.dot(a, b, preferred_element_type=f32)


def dot3(lefts, b):
    rows = [high.shape[0] for high, _ in lefts]
    highs = jnp.concatenate([high for high, _ in lefts], axis=0)
    both = dot(jnp.concatenate([highs] + [low for _, low in lefts], axis=0), b[0])
    side = dot(highs, b[1])
    outs, at, total = [], 0, sum(rows)
    for r in rows:
        outs.append(both[at : at + r] + (side[at : at + r] + both[total + at : total + at + r]))
        at += r
    return outs


def pack_body(live, grads, mom, mine, theirs, mine_wide, theirs_wide, count, rows, own_mom, holder, row_sems, mom_sem):
    slots, height, width = rows.shape
    mats = live.shape[0]
    fetch_mom = pltpu.make_async_copy(mom, own_mom, mom_sem)
    fetch_mom.start()
    for s in range(slots):
        holder[s] = 0
    found = 0
    for m in range(mats):
        holder[found] = m
        found = found + jnp.where(live[m] > 0, 1, 0)
    count[0] = found
    used = jnp.where(found > 16, slots, 16)

    def fetch(s):
        return pltpu.make_async_copy(grads.at[0, holder[s]], rows.at[s], row_sems.at[s])

    def begin(s, _):
        fetch(s).start()
        return 0

    lax.fori_loop(0, used, begin, 0)
    rep, x1 = lax.axis_index("rep"), lax.axis_index("x1")
    x0, c = lax.axis_index("x0"), lax.axis_index("c")
    group = lax.broadcasted_iota(i32, (height, 128), 1) // 32
    start = pl.multiple_of((rep * 2 + x1) * 128, 128)
    fetch_mom.wait()

    def spread(slots, block, near, far):
        blocks = width // block
        old = lax.broadcasted_iota(i32, (block, block), 0)
        new = lax.broadcasted_iota(i32, (block, block), 1)
        far_half = ((old // 32 % 2) ^ c) * (block // 2)
        if block == 512:
            target = far_half + (old // 64 % 2) * 128 + old // 128 * 32 + old % 32
        else:
            target = far_half + old // 128 * 64 + (old // 64 % 2) * 32 + old % 32
        deal = jnp.where(target == new, 1.0, 0.0).astype(bf16)

        def eight(g, _):
            lead = []
            for k in range(8):
                s = g * 8 + k
                fetch(s).wait()
                own = own_mom[holder[s]] * decay_rate
                own = jnp.concatenate([own] * 4, axis=1)
                at = (s, slice(None), pl.ds(start, 128))
                rows[at] = rows[at] + jnp.where(group == x0 * 2 + c, own, 0.0)
                for n in range(blocks):
                    lead.append(rows[s, :, n * block : (n + 1) * block].astype(bf16))
            dealt = dot(jnp.concatenate(lead, axis=0), deal).astype(bf16)
            for k in range(8):
                for n in range(blocks):
                    part = dealt[(k * blocks + n) * height : (k * blocks + n + 1) * height]
                    cols = slice(n * 128, (n + 1) * 128)
                    for h in range(block // 256):
                        to = (g * 8 + k) * (block // 256) + h
                        near[to, :, cols] = part[:, h * 128 : (h + 1) * 128]
                        far[to, :, cols] = part[:, block // 2 + h * 128 : block // 2 + (h + 1) * 128]
            return 0

        lax.fori_loop(0, slots // 8, eight, 0)

    pl.when(found <= 16)(lambda: spread(16, 512, mine, theirs))
    pl.when(found > 16)(lambda: spread(slots, 256, mine_wide, theirs_wide))


def pack(layer_live, grad_parts, momentum):
    _, _, rows, cols = grad_parts.shape
    half = jax.ShapeDtypeStruct((32, rows, cols // 4), bf16)
    wide = jax.ShapeDtypeStruct((32, rows, cols // 2), bf16)
    grad_parts = pltpu.with_memory_space_constraint(grad_parts, pltpu.HBM)
    momentum = pltpu.with_memory_space_constraint(momentum, pltpu.HBM)
    return pl.pallas_call(
        pack_body,
        in_specs=[whole(pltpu.SMEM), whole(pl.ANY), whole(pl.ANY)],
        out_specs=[whole()] * 4 + [whole(pltpu.SMEM)],
        out_shape=[half, half, wide, wide, jax.ShapeDtypeStruct((1,), i32)],
        scratch_shapes=[
            pltpu.VMEM((32, rows, cols), f32),
            pltpu.VMEM(momentum.shape, f32),
            pltpu.SMEM((32,), i32),
            pltpu.SemaphoreType.DMA((32,)),
            pltpu.SemaphoreType.DMA,
        ],
        compiler_params=room(16),
        name="pack",
    )(layer_live, grad_parts, momentum)


def total_body(parts, out):
    total = jnp.sum(parts[...].astype(f32), axis=0).astype(bf16)
    for z in range(out.shape[0]):
        out[z] = total


def total(parts, copies):
    return pl.pallas_call(
        total_body,
        in_specs=[whole()],
        out_specs=whole(),
        out_shape=jax.ShapeDtypeStruct((copies,) + parts.shape[1:], bf16),
        compiler_params=room(4),
        name="total",
    )(parts)


def gram_body(source, out):
    s = source[...].reshape(source.shape[0] * source.shape[1], -1)
    g = lax.dot_general(s, s, (((1,), (1,)), ((), ())), preferred_element_type=f32)
    out[:64] = g[:64]
    out[64:, 64:] = g[64:128, 64:]
    out[64:, :64] = g[128:, 128:]


def gram(source):
    return pl.pallas_call(
        gram_body,
        in_specs=[whole()],
        out_specs=whole(),
        out_shape=jax.ShapeDtypeStruct((128, 192), f32),
        compiler_params=room(4),
        name="gram",
    )(source)


def unfolded(g):
    top, low = g[:64], g[64:]
    middle = jnp.concatenate([top[:, 64:128].T, low[:, 64:]], axis=1)
    bottom = jnp.concatenate([top[:, 128:].T, low[:, 128:].T, low[:, :64]], axis=1)
    return jnp.concatenate([top, middle, bottom], axis=0)


def schulz_body(gram_a, gram_b, source, out):
    g = unfolded(gram_a[...] + gram_b[...])
    rows = g.shape[0]
    own_rows = source.shape[1]
    z = lax.axis_index("dp")
    row = lax.broadcasted_iota(i32, g.shape, 0)
    col = lax.broadcasted_iota(i32, g.shape, 1)
    eye = row == col
    square = jnp.sum(jnp.sum(jnp.where(eye, g, 0.0), axis=1, keepdims=True), axis=0, keepdims=True)
    scale = 1.0 / (jnp.sqrt(square) + norm_eps)
    g = g * scale * scale
    pick = (
        lax.broadcasted_iota(i32, (own_rows, rows), 1)
        == lax.broadcasted_iota(i32, (own_rows, rows), 0) + z * own_rows
    )
    gh = halves(g)
    lead = pick.astype(f32)
    for iteration in range(ITERS - 1):
        w = second_coef * g + third_coef * dot3([gh], gh)[0] + jnp.where(eye, first_coef, 0.0)
        wh = halves(w)
        turned = halves(dot3([wh], gh)[0])
        g, lead = dot3([turned, halves(lead)], wh)
        gh = halves(g)
    once = dot3([halves(lead)], gh)[0]
    twice = dot3([halves(once)], gh)[0]
    lead = first_coef * lead + second_coef * once + third_coef * twice
    lead = halves(lead * (scale * math.sqrt(2048.0)))
    s = source[...].reshape(rows, -1)
    result = dot(lead[0], s) + dot(lead[1], s)
    own = source[z].astype(f32)
    half = own_rows // 2
    group = lax.broadcasted_iota(i32, (half, 128), 1) // 32
    for j in range(out.shape[0]):
        yy, t = j // 4, j % 4
        piece = None
        for place_at, (whole_rows, first) in enumerate(((result, 0), (result, half), (own, 0), (own, half))):
            part = whole_rows[first : first + half, yy * 128 : (yy + 1) * 128]
            turn = (place_at - t) * 32 % 128
            part = pltpu.roll(part, turn, 1) if turn else part
            piece = part if piece is None else jnp.where(group == place_at, part, piece)
        out[j] = piece.astype(bf16)


def schulz(gram_a, gram_b, source):
    return pl.pallas_call(
        schulz_body,
        in_specs=[whole(), whole(), whole()],
        out_specs=whole(),
        out_shape=jax.ShapeDtypeStruct((source.shape[2] // 32, source.shape[1] // 2, 128), bf16),
        compiler_params=room(8),
        name="schulz",
    )(gram_a, gram_b, source)


def place_body(live, came, mom_in, mom, orth):
    found = 0
    for m in range(mom.shape[0]):
        here = live[m] > 0
        got = came[jnp.minimum(found, came.shape[0] - 1)].astype(f32)
        found = found + jnp.where(here, 1, 0)
        parts = [got[:, :32]] + [pltpu.roll(got, 128 - 32 * t, 1)[:, :32] for t in range(1, 4)]
        mom[m] = jnp.where(here, jnp.concatenate(parts[2:], axis=0), mom_in[m])
        orth[m] = jnp.where(here, jnp.concatenate(parts[:2], axis=0), 0.0).astype(bf16)


def place(layer_live, came, momentum):
    return pl.pallas_call(
        place_body,
        in_specs=[whole(pltpu.SMEM), whole(), whole()],
        out_specs=[whole(), whole()],
        out_shape=[jax.ShapeDtypeStruct(momentum.shape, f32), jax.ShapeDtypeStruct(momentum.shape, bf16)],
        compiler_params=room(4),
        name="place",
    )(layer_live, came, momentum)


def swapped(x, axis):
    return lax.ppermute(x, axis, [(0, 1), (1, 0)])


def finish(mine, came, wide, layer_live, momentum):
    chip_sum = (mine.astype(f32) + came.astype(f32)).astype(bf16)
    parts = lax.all_to_all(chip_sum, CHIPS, 0, 0, tiled=True)
    copies = total(parts, lax.axis_size("dp"))
    source = lax.all_to_all(copies, "dp", 0, 0, tiled=True)
    partial = gram(source)
    if wide:
        update = schulz(partial, swapped(partial, "c"), source)
        back = lax.all_to_all(update, CHIPS, 0, 0, tiled=True)
    else:
        partial = partial + swapped(partial, "c")
        update = schulz(partial, swapped(partial, "x0"), source)
        back = lax.all_to_all(update, OWNERS, 0, 0, tiled=True)
    return tuple(place(layer_live, back, momentum))


def per_device(grad_parts, momentum, layer_live):
    mine, theirs, mine_wide, theirs_wide, count = pack(layer_live, grad_parts, momentum)
    came = swapped(theirs, "c")

    def narrow(mine, came, mine_wide, theirs_wide, *rest):
        return finish(mine, came, False, *rest)

    def wide(mine, came, mine_wide, theirs_wide, *rest):
        return finish(mine_wide, swapped(theirs_wide, "c"), True, *rest)

    return lax.cond(count[0] > 16, wide, narrow, mine, came, mine_wide, theirs_wide, layer_live, momentum)


def solution(mesh):
    torus = Mesh(
        mesh.devices.reshape(mesh.shape["dp"], mesh.shape["rep"], 2, 2, 2),
        ("dp", "rep", "x1", "x0", "c"),
    )
    return jax.shard_map(
        per_device,
        mesh=torus,
        in_specs=(P(COLS, None, "dp", None), P(None, "dp", COLS), P()),
        out_specs=(P(None, "dp", COLS), P(None, "dp", COLS)),
        check_vma=False,
    )
```

profile of v0, /device:TPU:2, one launch (start us, length us, event | category | flops | bytes accessed | tf_op | source)
XLA Modules:
  0.0 95.3 jit_solution(13965199937125263336)
XLA Ops:
  0.6 0.0 copy-start.1
  0.6 0.0 copy-start
  0.6 5.0 %pack.1 = (bf16[32,16,512]{2,1,0:T(8,128)(2,1)S(1)}, bf16[32,16,512]{2,1,0:T(8,128)(2,1)S(1)}, bf16[32,16,1024]{2,1,0:T(8,128)(2,1)S(1)}, bf16[32,16,1024]{2,1,0:T(8,128)(2,1)S(1)}, s32[1]{0:T(128)}) custom-call(s32[24]{0:T(128)} %live.1, f32[1,24,16,2048]{3,2,1,0:T(8,128)} %grads.1, f32[24,16,32]{2,1,0:T(8,128)} %mom.1), custom_call_target="tpu_custom_call" | custom-call | tf_op jit(solution)/shard_map/pack/pallas_call | solution.py:130
  5.6 1.9 %collective-permute-start.4 = (bf16[32,16,512]{2,1,0:T(8,128)(2,1)S(1)}, bf16[32,16,512]{2,1,0:T(8,128)(2,1)S(1)}, u32[]{:S(2)}, u32[]{:S(2)}) collective-permute-start(bf16[32,16,512]{2,1,0:T(8,128)(2,1)S(1)} %get-tuple-element.33), channel_id=1, source_target_pairs={{0,1},{1,0},{2,3},{3,2},{4,5},{5,4},{6,7},{7,6},{8,9},{9,8},{10,11... | collective-permute-start | bytes 1572872 | tf_op jit(solution)/shard_map/ppermute | solution.py:267
  8.2 1.2 %collective-permute-done.4 = bf16[32,16,512]{2,1,0:T(8,128)(2,1)S(1)} collective-permute-done((bf16[32,16,512]{2,1,0:T(8,128)(2,1)S(1)}, bf16[32,16,512]{2,1,0:T(8,128)(2,1)S(1)}, u32[]{:S(2)}, u32[]{:S(2)}) %collective-permute-start.4) | collective-permute-done | bytes 524320 | tf_op jit(solution)/shard_map/ppermute | solution.py:267
  9.4 0.0 copy-done.1
  9.4 0.0 copy-done
  9.4 85.9 %conditional.1 = ((f32[24,16,32]{2,1,0:T(8,128)}, bf16[24,16,32]{2,1,0:T(8,128)(2,1)})) conditional(s32[]{:T(128)} %bitcast, (bf16[32,16,512]{2,1,0:T(8,128)(2,1)S(1)}, bf16[32,16,512]{2,1,0:T(8,128)(2,1)S(1)}, s32[24]{0:T(128)S(1)}, f32[24,16,32]{2,1,0:T(8,128)S(1)}) %tuple.25, (bf16[32,16,1024]{2,1,0:T(8,128)(2,1)S(1)}, ...), branch_computations={%region_0.0_spmd, %region_1.0_spmd} | conditional | flops 2097152 | bytes 10747992 | solution.py:296
  9.4 0.2 add_convert_fusion
  9.6 29.7 %all_to_all.24.parts = bf16[32,16,512]{2,1,0:T(8,128)(2,1)S(1)} all-to-all(bf16[32,16,512]{2,1,0:T(8,128)(2,1)S(1)} %add_convert_fusion), channel_id=1, replica_groups=mesh['dp'=12,'rep'=8,'x1'=2,'x0'=2,'c'=2] {'rep','x1','x0'}, dimensions={0} | all-to-all | bytes 1048576 | tf_op jit(solution)/shard_map/cond/branch_0_fun/all_to_all | solution.py:272
  39.3 0.1 total.2
  39.4 25.2 %all_to_all.25.source = bf16[12,16,512]{2,1,0:T(8,128)(2,1)S(1)} all-to-all(bf16[12,16,512]{2,1,0:T(8,128)(2,1)S(1)} %total.2), channel_id=1, replica_groups=mesh['dp'=12,'rep'=8,'x1'=2,'x0'=2,'c'=2] {'dp'}, dimensions={0} | all-to-all | bytes 393216 | tf_op jit(solution)/shard_map/cond/branch_0_fun/all_to_all | solution.py:274
  64.6 0.2 gram.2
  64.9 1.9 %collective-permute-start = (f32[128,192]{1,0:T(8,128)S(1)}, f32[128,192]{1,0:T(8,128)S(1)}, u32[]{:S(2)}, u32[]{:S(2)}) collective-permute-start(f32[128,192]{1,0:T(8,128)S(1)} %gram.2), channel_id=1, source_target_pairs={{0,1},{1,0},{2,3},{3,2},{4,5},{5,4},{6,7},{7,6},{8,9},{9,8},{10,11... | collective-permute-start | bytes 294920 | tf_op jit(solution)/shard_map/cond/branch_0_fun/ppermute | solution.py:267
  66.8 1.3 %collective-permute-done = f32[128,192]{1,0:T(8,128)S(1)} collective-permute-done((f32[128,192]{1,0:T(8,128)S(1)}, f32[128,192]{1,0:T(8,128)S(1)}, u32[]{:S(2)}, u32[]{:S(2)}) %collective-permute-start) | collective-permute-done | bytes 98336 | tf_op jit(solution)/shard_map/cond/branch_0_fun/ppermute | solution.py:267
  68.1 3.1 %collective-permute-start.1 = (f32[128,192]{1,0:T(8,128)S(1)}, f32[128,192]{1,0:T(8,128)S(1)}, u32[]{:S(2)}, u32[]{:S(2)}) collective-permute-start(f32[128,192]{1,0:T(8,128)S(1)} %add.7.gram_a), channel_id=1, source_target_pairs={{0,2},{2,0},{1,3},{3,1},{4,6},{6,4},{5,7},{7,5},{8,10},{10,8},{9,1... | collective-permute-start | bytes 294920 | tf_op jit(solution)/shard_map/cond/branch_0_fun/ppermute | solution.py:267
  71.2 4.3 %collective-permute-done.1.gram_b = f32[128,192]{1,0:T(8,128)S(1)} collective-permute-done((f32[128,192]{1,0:T(8,128)S(1)}, f32[128,192]{1,0:T(8,128)S(1)}, u32[]{:S(2)}, u32[]{:S(2)}) %collective-permute-start.1) | collective-permute-done | bytes 98336 | tf_op jit(solution)/shard_map/cond/branch_0_fun/ppermute | solution.py:267
  75.6 3.8 %schulz.2 = bf16[16,8,128]{2,1,0:T(8,128)(2,1)S(1)} custom-call(f32[128,192]{1,0:T(8,128)S(1)} %add.7.gram_a, f32[128,192]{1,0:T(8,128)S(1)} %collective-permute-done.1.gram_b, bf16[12,16,512]{2,1,0:T(8,128)(2,1)S(1)} %all_to_all.25.source), custom_call_target="tpu_custom_call" | custom-call | tf_op jit(solution)/shard_map/cond/branch_0_fun/schulz/pallas_call | solution.py:234
  79.4 14.6 %all_to_all.26.came = bf16[16,8,128]{2,1,0:T(8,128)(2,1)S(1)} all-to-all(bf16[16,8,128]{2,1,0:T(8,128)(2,1)S(1)} %schulz.2), channel_id=1, replica_groups=mesh['dp'=12,'rep'=8,'x1'=2,'x0'=2,'c'=2] {'rep','x1'}, dimensions={0} | all-to-all | bytes 65536 | tf_op jit(solution)/shard_map/cond/branch_0_fun/all_to_all | solution.py:282
  94.0 1.4 %place.2 = (f32[24,16,32]{2,1,0:T(8,128)}, bf16[24,16,32]{2,1,0:T(8,128)(2,1)}) custom-call(s32[24]{0:T(128)S(1)} %get-tuple-element.16.live, bf16[16,8,128]{2,1,0:T(8,128)(2,1)S(1)} %all_to_all.26.came, f32[24,16,32]{2,1,0:T(8,128)S(1)} %get-tuple-element.19.mom_in), custom_call_target="tpu_custom_call" | custom-call | tf_op jit(solution)/shard_map/cond/branch_0_fun/place/pallas_call | solution.py:256
  (1 shorter events, 0.0 us)
Async XLA Ops:
  0.6 8.8 %copy-start.1 = (s32[24]{0:T(128)S(1)}, s32[24]{0:T(128)}, u32[]{:S(2)}) copy-start(s32[24]{0:T(128)} %live.1) | copy-start | bytes 292
  0.6 8.8 %copy-start = (f32[24,16,32]{2,1,0:T(8,128)S(1)}, f32[24,16,32]{2,1,0:T(8,128)}, u32[]{:S(2)}) copy-start(f32[24,16,32]{2,1,0:T(8,128)} %mom.1) | copy-start | bytes 147460
  5.6 3.8 %collective-permute-start.4 = (bf16[32,16,512]{2,1,0:T(8,128)(2,1)S(1)}, bf16[32,16,512]{2,1,0:T(8,128)(2,1)S(1)}, u32[]{:S(2)}, u32[]{:S(2)}) collective-permute-start(bf16[32,16,512]{2,1,0:T(8,128)(2,1)S(1)} %get-tuple-element.33), channel_id=1, source_target_pairs={{0,1},{1,0},{2,3},{3,2},{4,5},{5,4},{6,7},{7,6},{8,9},{9,8},{10,11... | collective-permute-start | bytes 1572872 | tf_op jit(solution)/shard_map/ppermute | solution.py:267
  64.9 3.2 %collective-permute-start = (f32[128,192]{1,0:T(8,128)S(1)}, f32[128,192]{1,0:T(8,128)S(1)}, u32[]{:S(2)}, u32[]{:S(2)}) collective-permute-start(f32[128,192]{1,0:T(8,128)S(1)} %gram.2), channel_id=1, source_target_pairs={{0,1},{1,0},{2,3},{3,2},{4,5},{5,4},{6,7},{7,6},{8,9},{9,8},{10,11... | collective-permute-start | bytes 294920 | tf_op jit(solution)/shard_map/cond/branch_0_fun/ppermute | solution.py:267
  68.1 7.4 %collective-permute-start.1 = (f32[128,192]{1,0:T(8,128)S(1)}, f32[128,192]{1,0:T(8,128)S(1)}, u32[]{:S(2)}, u32[]{:S(2)}) collective-permute-start(f32[128,192]{1,0:T(8,128)S(1)} %add.7.gram_a), channel_id=1, source_target_pairs={{0,2},{2,0},{1,3},{3,1},{4,6},{6,4},{5,7},{7,5},{8,10},{10,8},{9,1... | collective-permute-start | bytes 294920 | tf_op jit(solution)/shard_map/cond/branch_0_fun/ppermute | solution.py:267
where the time goes:
time: 95.7 us; the launch traced here: 95.3 us
  blocking collectives  69.5 us (73%)
  Pallas kernels  10.4 us (11%)
  starting transfers between devices  6.95 us (7%)
  waiting for transfers between devices  6.87 us (7%)
  between operations  1.31 us (1%)
    all_to_all x1, blocking collectives, finish(): parts = lax.all_to_all(chip_sum, CHIPS, 0, 0, tiled=True)  29.7 us
    all_to_all x1, blocking collectives, finish(): source = lax.all_to_all(copies, 'dp', 0, 0, tiled=True)  25.2 us
    all_to_all x1, blocking collectives, finish(): back = lax.all_to_all(update, OWNERS, 0, 0, tiled=True)  14.6 us
    ppermute x3, starting transfers between devices, swapped(): return lax.ppermute(x, axis, [(0, 1), (1, 0)])  6.95 us
    ppermute x3, waiting for transfers between devices, swapped(): return lax.ppermute(x, axis, [(0, 1), (1, 0)])  6.87 us
    pallas_call x1, Pallas kernels, pack(): pl.pallas_call(pack_body, in_specs=[whole(pltpu.SMEM), whole(pl.ANY), who...  4.98 us
    pallas_call x1, Pallas kernels, schulz(): pl.pallas_call(schulz_body, in_specs=[whole(), whole(), whole()], out_spe...  3.78 us
  transfers between devices with their start and end apart: 3, of which 3 were waited for; matrix products, arithmetic and copies ran while one was open for 0% of the time, Pallas kernels for 0%

commit v1 on v0

--- a/solution.py
+++ b/solution.py
@@ -93,10 +93,10 @@
             target = far_half + old // 128 * 64 + (old // 64 % 2) * 32 + old % 32
         deal = jnp.where(target == new, 1.0, 0.0).astype(bf16)
 
-        def eight(g, _):
+        def sixteen(g, _):
             lead = []
-            for k in range(8):
-                s = g * 8 + k
+            for k in range(16):
+                s = g * 16 + k
                 fetch(s).wait()
                 own = own_mom[holder[s]] * decay_rate
                 own = jnp.concatenate([own] * 4, axis=1)
@@ -105,17 +105,17 @@
                 for n in range(blocks):
                     lead.append(rows[s, :, n * block : (n + 1) * block].astype(bf16))
             dealt = dot(jnp.concatenate(lead, axis=0), deal).astype(bf16)
-            for k in range(8):
+            for k in range(16):
                 for n in range(blocks):
                     part = dealt[(k * blocks + n) * height : (k * blocks + n + 1) * height]
                     cols = slice(n * 128, (n + 1) * 128)
                     for h in range(block // 256):
-                        to = (g * 8 + k) * (block // 256) + h
+                        to = (g * 16 + k) * (block // 256) + h
                         near[to, :, cols] = part[:, h * 128 : (h + 1) * 128]
                         far[to, :, cols] = part[:, block // 2 + h * 128 : block // 2 + (h + 1) * 128]
             return 0
 
-        lax.fori_loop(0, slots // 8, eight, 0)
+        lax.fori_loop(0, slots // 16, sixteen, 0)
 
     pl.when(found <= 16)(lambda: spread(16, 512, mine, theirs))
     pl.when(found > 16)(lambda: spread(slots, 256, mine_wide, theirs_wide))

time: 95.7 us -> 95.6 us (level)
  no operation moved by 1% of the time
where the time goes in v1:
time: 95.6 us; the launch traced here: 95.2 us
  blocking collectives  69.5 us (73%)
  Pallas kernels  10.3 us (11%)
  starting transfers between devices  6.95 us (7%)
  waiting for transfers between devices  6.87 us (7%)
  between operations  1.31 us (1%)
    all_to_all x1, blocking collectives, finish(): parts = lax.all_to_all(chip_sum, CHIPS, 0, 0, tiled=True)  29.7 us
    all_to_all x1, blocking collectives, finish(): source = lax.all_to_all(copies, 'dp', 0, 0, tiled=True)  25.3 us
    all_to_all x1, blocking collectives, finish(): back = lax.all_to_all(update, OWNERS, 0, 0, tiled=True)  14.6 us
    ppermute x3, starting transfers between devices, swapped(): return lax.ppermute(x, axis, [(0, 1), (1, 0)])  6.95 us
    ppermute x3, waiting for transfers between devices, swapped(): return lax.ppermute(x, axis, [(0, 1), (1, 0)])  6.87 us
    pallas_call x1, Pallas kernels, pack(): pl.pallas_call(pack_body, in_specs=[whole(pltpu.SMEM), whole(pl.ANY), who...  4.88 us
    pallas_call x1, Pallas kernels, schulz(): pl.pallas_call(schulz_body, in_specs=[whole(), whole(), whole()], out_spe...  3.78 us
  transfers between devices with their start and end apart: 3, of which 3 were waited for; matrix products, arithmetic and copies ran while one was open for 0% of the time, Pallas kernels for 0%

profile of v1, /device:TPU:2, one launch (start us, length us, event | category | flops | bytes accessed | tf_op | source)
XLA Modules:
  0.0 95.2 jit_solution(4707847534678909722)
XLA Ops:
  0.6 0.0 copy-start.1
  0.6 0.0 copy-start
  0.6 4.9 %pack.1 = (bf16[32,16,512]{2,1,0:T(8,128)(2,1)S(1)}, bf16[32,16,512]{2,1,0:T(8,128)(2,1)S(1)}, bf16[32,16,1024]{2,1,0:T(8,128)(2,1)S(1)}, bf16[32,16,1024]{2,1,0:T(8,128)(2,1)S(1)}, s32[1]{0:T(128)}) custom-call(s32[24]{0:T(128)} %live.1, f32[1,24,16,2048]{3,2,1,0:T(8,128)} %grads.1, f32[24,16,32]{2,1,0:T(8,128)} %mom.1), custom_call_target="tpu_custom_call" | custom-call | tf_op jit(solution)/shard_map/pack/pallas_call | solution.py:130
  5.5 1.9 %collective-permute-start.4 = (bf16[32,16,512]{2,1,0:T(8,128)(2,1)S(1)}, bf16[32,16,512]{2,1,0:T(8,128)(2,1)S(1)}, u32[]{:S(2)}, u32[]{:S(2)}) collective-permute-start(bf16[32,16,512]{2,1,0:T(8,128)(2,1)S(1)} %get-tuple-element.33), channel_id=1, source_target_pairs={{0,1},{1,0},{2,3},{3,2},{4,5},{5,4},{6,7},{7,6},{8,9},{9,8},{10,11... | collective-permute-start | bytes 1572872 | tf_op jit(solution)/shard_map/ppermute | solution.py:267
  8.1 1.2 %collective-permute-done.4 = bf16[32,16,512]{2,1,0:T(8,128)(2,1)S(1)} collective-permute-done((bf16[32,16,512]{2,1,0:T(8,128)(2,1)S(1)}, bf16[32,16,512]{2,1,0:T(8,128)(2,1)S(1)}, u32[]{:S(2)}, u32[]{:S(2)}) %collective-permute-start.4) | collective-permute-done | bytes 524320 | tf_op jit(solution)/shard_map/ppermute | solution.py:267
  9.3 0.0 copy-done.1
  9.3 0.0 copy-done
  9.3 85.9 %conditional.1 = ((f32[24,16,32]{2,1,0:T(8,128)}, bf16[24,16,32]{2,1,0:T(8,128)(2,1)})) conditional(s32[]{:T(128)} %bitcast, (bf16[32,16,512]{2,1,0:T(8,128)(2,1)S(1)}, bf16[32,16,512]{2,1,0:T(8,128)(2,1)S(1)}, s32[24]{0:T(128)S(1)}, f32[24,16,32]{2,1,0:T(8,128)S(1)}) %tuple.25, (bf16[32,16,1024]{2,1,0:T(8,128)(2,1)S(1)}, ...), branch_computations={%region_0.0_spmd, %region_1.0_spmd} | conditional | flops 2097152 | bytes 10747992 | solution.py:296
  9.3 0.2 add_convert_fusion
  9.5 29.7 %all_to_all.24.parts = bf16[32,16,512]{2,1,0:T(8,128)(2,1)S(1)} all-to-all(bf16[32,16,512]{2,1,0:T(8,128)(2,1)S(1)} %add_convert_fusion), channel_id=1, replica_groups=mesh['dp'=12,'rep'=8,'x1'=2,'x0'=2,'c'=2] {'rep','x1','x0'}, dimensions={0} | all-to-all | bytes 1048576 | tf_op jit(solution)/shard_map/cond/branch_0_fun/all_to_all | solution.py:272
  39.2 0.1 total.2
  39.3 25.3 %all_to_all.25.source = bf16[12,16,512]{2,1,0:T(8,128)(2,1)S(1)} all-to-all(bf16[12,16,512]{2,1,0:T(8,128)(2,1)S(1)} %total.2), channel_id=1, replica_groups=mesh['dp'=12,'rep'=8,'x1'=2,'x0'=2,'c'=2] {'dp'}, dimensions={0} | all-to-all | bytes 393216 | tf_op jit(solution)/shard_map/cond/branch_0_fun/all_to_all | solution.py:274
  64.5 0.2 gram.2
  64.8 1.9 %collective-permute-start = (f32[128,192]{1,0:T(8,128)S(1)}, f32[128,192]{1,0:T(8,128)S(1)}, u32[]{:S(2)}, u32[]{:S(2)}) collective-permute-start(f32[128,192]{1,0:T(8,128)S(1)} %gram.2), channel_id=1, source_target_pairs={{0,1},{1,0},{2,3},{3,2},{4,5},{5,4},{6,7},{7,6},{8,9},{9,8},{10,11... | collective-permute-start | bytes 294920 | tf_op jit(solution)/shard_map/cond/branch_0_fun/ppermute | solution.py:267
  66.7 1.3 %collective-permute-done = f32[128,192]{1,0:T(8,128)S(1)} collective-permute-done((f32[128,192]{1,0:T(8,128)S(1)}, f32[128,192]{1,0:T(8,128)S(1)}, u32[]{:S(2)}, u32[]{:S(2)}) %collective-permute-start) | collective-permute-done | bytes 98336 | tf_op jit(solution)/shard_map/cond/branch_0_fun/ppermute | solution.py:267
  68.0 3.1 %collective-permute-start.1 = (f32[128,192]{1,0:T(8,128)S(1)}, f32[128,192]{1,0:T(8,128)S(1)}, u32[]{:S(2)}, u32[]{:S(2)}) collective-permute-start(f32[128,192]{1,0:T(8,128)S(1)} %add.7.gram_a), channel_id=1, source_target_pairs={{0,2},{2,0},{1,3},{3,1},{4,6},{6,4},{5,7},{7,5},{8,10},{10,8},{9,1... | collective-permute-start | bytes 294920 | tf_op jit(solution)/shard_map/cond/branch_0_fun/ppermute | solution.py:267
  71.1 4.3 %collective-permute-done.1.gram_b = f32[128,192]{1,0:T(8,128)S(1)} collective-permute-done((f32[128,192]{1,0:T(8,128)S(1)}, f32[128,192]{1,0:T(8,128)S(1)}, u32[]{:S(2)}, u32[]{:S(2)}) %collective-permute-start.1) | collective-permute-done | bytes 98336 | tf_op jit(solution)/shard_map/cond/branch_0_fun/ppermute | solution.py:267
  75.5 3.8 %schulz.2 = bf16[16,8,128]{2,1,0:T(8,128)(2,1)S(1)} custom-call(f32[128,192]{1,0:T(8,128)S(1)} %add.7.gram_a, f32[128,192]{1,0:T(8,128)S(1)} %collective-permute-done.1.gram_b, bf16[12,16,512]{2,1,0:T(8,128)(2,1)S(1)} %all_to_all.25.source), custom_call_target="tpu_custom_call" | custom-call | tf_op jit(solution)/shard_map/cond/branch_0_fun/schulz/pallas_call | solution.py:234
  79.3 14.6 %all_to_all.26.came = bf16[16,8,128]{2,1,0:T(8,128)(2,1)S(1)} all-to-all(bf16[16,8,128]{2,1,0:T(8,128)(2,1)S(1)} %schulz.2), channel_id=1, replica_groups=mesh['dp'=12,'rep'=8,'x1'=2,'x0'=2,'c'=2] {'rep','x1'}, dimensions={0} | all-to-all | bytes 65536 | tf_op jit(solution)/shard_map/cond/branch_0_fun/all_to_all | solution.py:282
  93.9 1.4 %place.2 = (f32[24,16,32]{2,1,0:T(8,128)}, bf16[24,16,32]{2,1,0:T(8,128)(2,1)}) custom-call(s32[24]{0:T(128)S(1)} %get-tuple-element.16.live, bf16[16,8,128]{2,1,0:T(8,128)(2,1)S(1)} %all_to_all.26.came, f32[24,16,32]{2,1,0:T(8,128)S(1)} %get-tuple-element.19.mom_in), custom_call_target="tpu_custom_call" | custom-call | tf_op jit(solution)/shard_map/cond/branch_0_fun/place/pallas_call | solution.py:256
  (1 shorter events, 0.0 us)
Async XLA Ops:
  0.6 8.7 %copy-start.1 = (s32[24]{0:T(128)S(1)}, s32[24]{0:T(128)}, u32[]{:S(2)}) copy-start(s32[24]{0:T(128)} %live.1) | copy-start | bytes 292
  0.6 8.7 %copy-start = (f32[24,16,32]{2,1,0:T(8,128)S(1)}, f32[24,16,32]{2,1,0:T(8,128)}, u32[]{:S(2)}) copy-start(f32[24,16,32]{2,1,0:T(8,128)} %mom.1) | copy-start | bytes 147460
  5.5 3.8 %collective-permute-start.4 = (bf16[32,16,512]{2,1,0:T(8,128)(2,1)S(1)}, bf16[32,16,512]{2,1,0:T(8,128)(2,1)S(1)}, u32[]{:S(2)}, u32[]{:S(2)}) collective-permute-start(bf16[32,16,512]{2,1,0:T(8,128)(2,1)S(1)} %get-tuple-element.33), channel_id=1, source_target_pairs={{0,1},{1,0},{2,3},{3,2},{4,5},{5,4},{6,7},{7,6},{8,9},{9,8},{10,11... | collective-permute-start | bytes 1572872 | tf_op jit(solution)/shard_map/ppermute | solution.py:267
  64.8 3.2 %collective-permute-start = (f32[128,192]{1,0:T(8,128)S(1)}, f32[128,192]{1,0:T(8,128)S(1)}, u32[]{:S(2)}, u32[]{:S(2)}) collective-permute-start(f32[128,192]{1,0:T(8,128)S(1)} %gram.2), channel_id=1, source_target_pairs={{0,1},{1,0},{2,3},{3,2},{4,5},{5,4},{6,7},{7,6},{8,9},{9,8},{10,11... | collective-permute-start | bytes 294920 | tf_op jit(solution)/shard_map/cond/branch_0_fun/ppermute | solution.py:267
  68.0 7.4 %collective-permute-start.1 = (f32[128,192]{1,0:T(8,128)S(1)}, f32[128,192]{1,0:T(8,128)S(1)}, u32[]{:S(2)}, u32[]{:S(2)}) collective-permute-start(f32[128,192]{1,0:T(8,128)S(1)} %add.7.gram_a), channel_id=1, source_target_pairs={{0,2},{2,0},{1,3},{3,1},{4,6},{6,4},{5,7},{7,5},{8,10},{10,8},{9,1... | collective-permute-start | bytes 294920 | tf_op jit(solution)/shard_map/cond/branch_0_fun/ppermute | solution.py:267
